TPU v7x, 32 devices: a whole 2x2x4 slice. The times are simulated.
32 devices in a mesh: gx: 4 (over y, core), gy: 4 (over z), gz: 2 (over x).
Axes of the slice: x: 2, y: 2, z: 4, core: 2. Of those that a mesh axis runs over, the one named last changes fastest.
Arguments:
- grads: bfloat16 [32, 4, 1, 8, 3584], P(('gx', 'gy', 'gz')), may hold values from -1196032 to 1196032
- counts: int32 [32], P(('gx', 'gy', 'gz')), may hold values from 1 to 4
- total_tokens: int32 [1], replicated, may hold values from 4000000 to 15999999
- master: float32 [1, 8, 3584], P(None, 'gy', ('gx', 'gz')), may hold values from -6 to 6
- moment1: float32 [1, 8, 3584], P(None, 'gy', ('gx', 'gz')), may hold values from -2 to 2
- moment2: float32 [1, 8, 3584], P(None, 'gy', ('gx', 'gz')), may hold values from 0.01 to 1
Outputs:
- params: bfloat16 [1, 8, 3584], replicated
- master_out: float32 [1, 8, 3584], P(None, 'gy', ('gx', 'gz'))
- moment1_out: float32 [1, 8, 3584], P(None, 'gy', ('gx', 'gz'))
- moment2_out: float32 [1, 8, 3584], P(None, 'gy', ('gx', 'gz'))
All inputs are finite; a program needn't handle non-finite values.
Results may differ from a plain program's by a relative error of at most 0.0004.
Values may be sent and summed in bfloat16 or wider, within the bound.
A program may use at most 64 MiB of HBM per device.

v0:
```python
import jax
import jax.numpy as jnp
from jax import lax
from jax.sharding import PartitionSpec as P


def body(grads, counts, total_tokens, master, moment1, moment2):
    rank_grads = grads[0]
    slots = jnp.arange(rank_grads.shape[0], dtype=jnp.int32)
    weights = (slots < counts[0]).astype(jnp.float32)
    accumulated = jnp.zeros(rank_grads.shape[1:], jnp.float32)
    for slot in range(rank_grads.shape[0]):
        accumulated = accumulated + weights[slot] * rank_grads[slot].astype(jnp.float32)
    partial_value = lax.psum_scatter(accumulated, ("gx", "gz"), scatter_dimension=2, tiled=True)
    summed = lax.psum_scatter(partial_value, "gy", scatter_dimension=1, tiled=True)
    gradient = summed / total_tokens.astype(jnp.float32)[0]
    moment1_out = 0.9 * moment1 + 0.1 * gradient
    moment2_out = 0.95 * moment2 + 0.05 * gradient * gradient
    first_fix = 1.0 - 0.9**10
    second_fix = 1.0 - 0.95**10
    update = moment1_out / first_fix / (jnp.sqrt(moment2_out / second_fix) + 1e-08)
    master_out = master - 0.01 * (update + 0.1 * master)
    shard_params = master_out.astype(jnp.bfloat16)
    wide_params = lax.all_gather(shard_params, ("gx", "gz"), axis=2, tiled=True)
    params = lax.all_gather(wide_params, "gy", axis=1, tiled=True)
    return (params, master_out, moment1_out, moment2_out)


def solution(mesh):
    return jax.shard_map(
        body,
        mesh=mesh,
        in_specs=(
            P(("gx", "gy", "gz"), None, None, None, None),
            P(("gx", "gy", "gz")),
            P(),
            P(None, "gy", ("gx", "gz")),
            P(None, "gy", ("gx", "gz")),
            P(None, "gy", ("gx", "gz")),
        ),
        out_specs=(
            P(),
            P(None, "gy", ("gx", "gz")),
            P(None, "gy", ("gx", "gz")),
            P(None, "gy", ("gx", "gz")),
        ),
        check_vma=False,
    )
```

profile of v0, /device:TPU:0, one launch (start us, length us, event | category | flops | bytes accessed | tf_op | source)
XLA Modules:
  0.0 125.8 jit_solution(12063351168490614243)
XLA Ops:
  7.2 0.0 reduce-scatter.5.cloned.1.call-start
  7.9 0.6 fusion.3
  8.5 3.5 %add_bitcast_fusion = f32[1,8,3584]{2,1,0:T(8,128)S(1)} fusion(bf16[1,4,1,8,3584]{4,3,2,1,0:T(8,128)(2,1)} %param.6, f32[]{:T(128)} %bitcast.8, f32[]{:T(128)} %bitcast.7, f32[]{:T(128)} %bitcast.6, f32[]{:T(128)} %bitcast.5), kind=kLoop, calls=%fused_computation | loop fusion | flops 315392 | bytes 344080 | tf_op jit(solution)/shard_map/add | solution.py:13
  12.0 0.0 copy-start.3
  12.0 0.0 copy-start
  12.0 0.0 copy-start.1
  12.0 0.0 copy-start.2
  12.0 3.0 %copy.13 = f32[1,8,3584]{1,0,2:T(1,128)} copy(f32[1,8,3584]{2,1,0:T(8,128)S(1)} %add_bitcast_fusion) | data formatting | bytes 229376
  15.0 0.0 reduce-scatter.5.cloned.1.call-update
  15.7 0.0 copy-done.3
  15.7 0.6 dynamic-slice
  17.0 40.5 %reduce-scatter.5.cloned.1.call-done = f32[448,8]{1,0:T(8,128)} async-done(((f32[3584,8]{1,0:T(8,128)}), f32[448,8]{1,0:T(8,128)}) %reduce-scatter.5.cloned.1.call-update) | async-done | bytes 14352
  57.5 1.0 copy.14
  58.5 18.7 %all-reduce = f32[1,8,448]{2,1,0:T(8,128)S(1)} all-reduce(f32[1,8,448]{2,1,0:T(8,128)S(1)} %copy.14), channel_id=3, replica_groups=mesh['gx'=4,'gy'=4,'gz'=2] {'gy'}, use_global_device_ids=true, to_apply=%region_1.0.clone | all-reduce | flops 3584 | bytes 28672
  77.2 0.0 copy-done
  77.2 0.0 copy-done.1
  77.2 0.0 copy-done.2
  77.3 0.6 fusion.1
  77.9 0.2 copy.10
  78.1 24.8 %all_gather.6 = bf16[1,2,3584]{1,0,2:T(2,128)(2,1)S(1)} all-gather(bf16[1,2,448]{1,0,2:T(2,128)(2,1)S(1)} %copy.10), channel_id=1, replica_groups=mesh['gx'=4,'gy'=4,'gz'=2] {'gx','gz'}, dimensions={2}, use_global_device_ids=true | all-gather | bytes 16128 | tf_op jit(solution)/shard_map/all_gather | solution.py:24
  102.9 2.0 %copy.11 = bf16[1,2,3584]{2,0,1:T(2,128)(2,1)S(1)} copy(bf16[1,2,3584]{1,0,2:T(2,128)(2,1)S(1)} %all_gather.6) | data formatting | bytes 28672 | tf_op jit(solution)/shard_map/all_gather | solution.py:24
  104.9 13.4 %all_gather.7 = bf16[1,8,3584]{2,0,1:T(2,128)(2,1)S(1)} all-gather(bf16[1,2,3584]{2,0,1:T(2,128)(2,1)S(1)} %copy.11), channel_id=1, replica_groups=mesh['gx'=4,'gy'=4,'gz'=2] {'gy'}, dimensions={1}, use_global_device_ids=true | all-gather | bytes 71680 | tf_op jit(solution)/shard_map/all_gather | solution.py:25
  118.3 0.6 copy.12
  (1 shorter events, 0.0 us)
Async XLA Ops:
  7.2 50.3 %reduce-scatter.5.cloned.1.call-start = ((), (), s32[]{:S(2)}) async-start(), calls=%async_computation.1 | async-start | bytes 2064384
  12.0 3.7 %copy-start.3 = (u32[32]{0:T(128)S(1)}, u32[32]{0:T(128)}, u32[]{:S(2)}) copy-start(u32[32]{0:T(128)} %constant.25) | copy-start | bytes 388
  12.0 65.2 %copy-start = (f32[1,2,448]{2,1,0:T(2,128)S(1)}, f32[1,2,448]{2,1,0:T(2,128)}, u32[]{:S(2)}) copy-start(f32[1,2,448]{2,1,0:T(2,128)} %param.9) | copy-start | bytes 10756
  12.0 65.2 %copy-start.1 = (f32[1,2,448]{2,1,0:T(2,128)S(1)}, f32[1,2,448]{2,1,0:T(2,128)}, u32[]{:S(2)}) copy-start(f32[1,2,448]{2,1,0:T(2,128)} %param.10) | copy-start | bytes 10756
  12.0 65.2 %copy-start.2 = (f32[1,2,448]{2,1,0:T(2,128)S(1)}, f32[1,2,448]{2,1,0:T(2,128)}, u32[]{:S(2)}) copy-start(f32[1,2,448]{2,1,0:T(2,128)} %param.11) | copy-start | bytes 10756
Sparse Core Ops, SparseCore 0:
  15.2 42.2 reduce-scatter.4
where the time goes:
time: 126 us
  blocking collectives  57 us (45%)
  waiting for transfers between devices  40.5 us (32%)
  between operations  16.1 us (13%)
  local copies, waits for them, and re-layouts  8.05 us (6%)
  other arithmetic  4.17 us (3%)
    unnamed x2, waiting for transfers between devices  40.5 us
    all_gather x1, blocking collectives, body(): wide_params = lax.all_gather(shard_params, ('gx', 'gz'), axis=2, tiled=True)  24.8 us
    unnamed x1, blocking collectives  18.7 us
    all_gather x1, blocking collectives, body(): params = lax.all_gather(wide_params, 'gy', axis=1, tiled=True)  13.4 us
    unnamed x12, local copies, waits for them, and re-layouts  5.27 us
    add x1, other arithmetic, body(): accumulated + weights[slot] * rank_grads[slot].astype(jnp.float32)  3.53 us
  transfers between devices with their start and end apart: 1, of which 1 were waited for; matrix products, arithmetic and copies ran while one was open for 0% of the time, Pallas kernels for 0%

commit v1 on v0

--- a/solution.py
+++ b/solution.py
@@ -22,7 +22,15 @@
     master_out = master - 0.01 * (update + 0.1 * master)
     shard_params = master_out.astype(jnp.bfloat16)
     wide_params = lax.all_gather(shard_params, ("gx", "gz"), axis=2, tiled=True)
-    params = lax.all_gather(wide_params, "gy", axis=1, tiled=True)
+    total_devices = jax.lax.psum(1, "gy")
+    pile = [wide_params]
+    for s in range(total_devices - 1):
+        step_out = jax.lax.ppermute(
+            pile[-1], "gy", [(c, (c + 1) % total_devices) for c in range(total_devices)]
+        )
+        pile.append(step_out)
+    earlier = jnp.concatenate(pile[::-1], 1)
+    params = jnp.roll(earlier, (jax.lax.axis_index("gy") + 1) * wide_params.shape[1], 1)
     return (params, master_out, moment1_out, moment2_out)
 
 

time: 126 us -> 129 us (1.024)
  waiting for transfers between devices: 40.5 us -> 57.1 us
  blocking collectives: 57 us -> 43.6 us
    ppermute x0 -> x3, waiting for transfers between devices: none -> 16.5 us  [body(): jax.lax.ppermute(pile[-1], 'gy', [(c, (c + 1) % total_devices) for c in r...]
    all_gather x1 -> x0, blocking collectives: 13.4 us -> none  [body(): params = lax.all_gather(wide_params, 'gy', axis=1, tiled=True)]
    unnamed x12 -> x11, local copies, waits for them, and re-layouts: 5.27 us -> 4.63 us
  transfers between devices with their start and end apart: 1 -> 4, of which waited for: 1 -> 4; matrix products, arithmetic and copies ran while one was open for 0% -> 0% of each run, Pallas kernels for 0% -> 0%
where the time goes in v1:
time: 129 us
  waiting for transfers between devices  57.1 us (44%)
  blocking collectives  43.6 us (34%)
  between operations  16.1 us (12%)
  local copies, waits for them, and re-layouts  8 us (6%)
  other arithmetic  4.17 us (3%)
    unnamed x2, waiting for transfers between devices  40.5 us
    all_gather x1, blocking collectives, body(): wide_params = lax.all_gather(shard_params, ('gx', 'gz'), axis=2, tiled=True)  24.8 us
    unnamed x1, blocking collectives  18.7 us
    ppermute x3, waiting for transfers between devices, body(): jax.lax.ppermute(pile[-1], 'gy', [(c, (c + 1) % total_devices) for c in r...  16.5 us
    unnamed x11, local copies, waits for them, and re-layouts  4.63 us
    add x1, other arithmetic, body(): accumulated + weights[slot] * rank_grads[slot].astype(jnp.float32)  3.53 us
  transfers between devices with their start and end apart: 4, of which 4 were waited for; matrix products, arithmetic and copies ran while one was open for 0% of the time, Pallas kernels for 0%

profile of v1, /device:TPU:0, one launch (start us, length us, event | category | flops | bytes accessed | tf_op | source)
XLA Modules:
  0.0 129.0 jit_solution(9101140034016788427)
XLA Ops:
  7.2 0.0 reduce-scatter.5.cloned.1.call-start
  7.9 0.6 fusion.3
  8.5 3.5 %add_bitcast_fusion = f32[1,8,3584]{2,1,0:T(8,128)S(1)} fusion(bf16[1,4,1,8,3584]{4,3,2,1,0:T(8,128)(2,1)} %param.6, f32[]{:T(128)} %bitcast.8, f32[]{:T(128)} %bitcast.7, f32[]{:T(128)} %bitcast.6, f32[]{:T(128)} %bitcast.5), kind=kLoop, calls=%fused_computation | loop fusion | flops 315392 | bytes 344080 | tf_op jit(solution)/shard_map/add | solution.py:13
  12.0 0.0 copy-start.3
  12.0 0.0 copy-start
  12.0 0.0 copy-start.1
  12.0 0.0 copy-start.2
  12.0 3.0 %copy.16 = f32[1,8,3584]{1,0,2:T(1,128)} copy(f32[1,8,3584]{2,1,0:T(8,128)S(1)} %add_bitcast_fusion) | data formatting | bytes 229376
  15.0 0.0 reduce-scatter.5.cloned.1.call-update
  15.7 0.0 copy-done.3
  15.7 0.6 dynamic-slice
  17.0 40.5 %reduce-scatter.5.cloned.1.call-done = f32[448,8]{1,0:T(8,128)} async-done(((f32[3584,8]{1,0:T(8,128)}), f32[448,8]{1,0:T(8,128)}) %reduce-scatter.5.cloned.1.call-update) | async-done | bytes 14352
  57.5 1.0 copy.17
  58.5 18.7 %all-reduce = f32[1,8,448]{2,1,0:T(8,128)S(1)} all-reduce(f32[1,8,448]{2,1,0:T(8,128)S(1)} %copy.17), channel_id=3, replica_groups=mesh['gx'=4,'gy'=4,'gz'=2] {'gy'}, use_global_device_ids=true, to_apply=%region_1.0.clone | all-reduce | flops 3584 | bytes 28672
  77.2 0.0 copy-done
  77.2 0.0 copy-done.1
  77.2 0.0 copy-done.2
  77.2 0.6 fusion.1
  77.9 0.2 copy.12
  78.1 24.8 %all_gather.3 = bf16[1,2,3584]{1,0,2:T(2,128)(2,1)S(1)} all-gather(bf16[1,2,448]{1,0,2:T(2,128)(2,1)S(1)} %copy.12), channel_id=1, replica_groups=mesh['gx'=4,'gy'=4,'gz'=2] {'gx','gz'}, dimensions={2}, use_global_device_ids=true | all-gather | bytes 16128 | tf_op jit(solution)/shard_map/all_gather | solution.py:24
  102.9 1.8 %copy.13 = bf16[1,2,3584]{2,1,0:T(2,128)(2,1)S(1)} copy(bf16[1,2,3584]{1,0,2:T(2,128)(2,1)S(1)} %all_gather.3) | data formatting | bytes 28672 | tf_op jit(solution)/shard_map/all_gather | solution.py:24
  104.7 0.1 collective-permute-start
  104.8 5.5 %collective-permute-done = bf16[1,2,3584]{2,1,0:T(2,128)(2,1)S(1)} collective-permute-done((bf16[1,2,3584]{2,1,0:T(2,128)(2,1)S(1)}, bf16[1,2,3584]{2,1,0:T(2,128)(2,1)S(1)}, u32[]{:S(2)}, u32[]{:S(2)}) %collective-permute-start) | collective-permute-done | bytes 14368 | tf_op jit(solution)/shard_map/ppermute | solution.py:28
  110.3 0.0 collective-permute-start.1
  110.3 5.5 %collective-permute-done.1 = bf16[1,2,3584]{2,1,0:T(2,128)(2,1)S(1)} collective-permute-done((bf16[1,2,3584]{2,1,0:T(2,128)(2,1)S(1)}, bf16[1,2,3584]{2,1,0:T(2,128)(2,1)S(1)}, u32[]{:S(2)}, u32[]{:S(2)}) %collective-permute-start.1) | collective-permute-done | bytes 14368 | tf_op jit(solution)/shard_map/ppermute | solution.py:28
  115.8 0.0 collective-permute-start.2
  115.8 5.5 %collective-permute-done.2 = bf16[1,2,3584]{2,1,0:T(2,128)(2,1)S(1)} collective-permute-done((bf16[1,2,3584]{2,1,0:T(2,128)(2,1)S(1)}, bf16[1,2,3584]{2,1,0:T(2,128)(2,1)S(1)}, u32[]{:S(2)}, u32[]{:S(2)}) %collective-permute-start.2) | collective-permute-done | bytes 14368 | tf_op jit(solution)/shard_map/ppermute | solution.py:28
  121.3 0.2 concatenate.6
  121.5 0.7 constant_dynamic-slice_fusion
  (1 shorter events, 0.0 us)
Async XLA Ops:
  7.2 50.3 %reduce-scatter.5.cloned.1.call-start = ((), (), s32[]{:S(2)}) async-start(), calls=%async_computation.1 | async-start | bytes 2064384
  12.0 3.7 %copy-start.3 = (u32[32]{0:T(128)S(1)}, u32[32]{0:T(128)}, u32[]{:S(2)}) copy-start(u32[32]{0:T(128)} %constant.57) | copy-start | bytes 388
  12.0 65.2 %copy-start = (f32[1,2,448]{2,1,0:T(2,128)S(1)}, f32[1,2,448]{2,1,0:T(2,128)}, u32[]{:S(2)}) copy-start(f32[1,2,448]{2,1,0:T(2,128)} %param.9) | copy-start | bytes 10756
  12.0 65.2 %copy-start.1 = (f32[1,2,448]{2,1,0:T(2,128)S(1)}, f32[1,2,448]{2,1,0:T(2,128)}, u32[]{:S(2)}) copy-start(f32[1,2,448]{2,1,0:T(2,128)} %param.10) | copy-start | bytes 10756
  12.0 65.2 %copy-start.2 = (f32[1,2,448]{2,1,0:T(2,128)S(1)}, f32[1,2,448]{2,1,0:T(2,128)}, u32[]{:S(2)}) copy-start(f32[1,2,448]{2,1,0:T(2,128)} %param.11) | copy-start | bytes 10756
  104.7 5.6 %collective-permute-start = (bf16[1,2,3584]{2,1,0:T(2,128)(2,1)S(1)}, bf16[1,2,3584]{2,1,0:T(2,128)(2,1)S(1)}, u32[]{:S(2)}, u32[]{:S(2)}) collective-permute-start(bf16[1,2,3584]{2,1,0:T(2,128)(2,1)S(1)} %copy.13), channel_id=1, source_target_pairs={{0,2},{2,4},{4,6},{6,0},{1,3},{3,5},{5,7},{7,1},{8,10},{10,12},{12... | collective-permute-start | bytes 43016 | tf_op jit(solution)/shard_map/ppermute | solution.py:28
  110.3 5.5 %collective-permute-start.1 = (bf16[1,2,3584]{2,1,0:T(2,128)(2,1)S(1)}, bf16[1,2,3584]{2,1,0:T(2,128)(2,1)S(1)}, u32[]{:S(2)}, u32[]{:S(2)}) collective-permute-start(bf16[1,2,3584]{2,1,0:T(2,128)(2,1)S(1)} %collective-permute-done), channel_id=1, source_target_pairs={{0,2},{2,4},{4,6},{6,0},{1,3},{3,5},{5,7},{7,1},{8,10},{10,12},{12... | collective-permute-start | bytes 43016 | tf_op jit(solution)/shard_map/ppermute | solution.py:28
  115.8 5.5 %collective-permute-start.2 = (bf16[1,2,3584]{2,1,0:T(2,128)(2,1)S(1)}, bf16[1,2,3584]{2,1,0:T(2,128)(2,1)S(1)}, u32[]{:S(2)}, u32[]{:S(2)}) collective-permute-start(bf16[1,2,3584]{2,1,0:T(2,128)(2,1)S(1)} %collective-permute-done.1), channel_id=1, source_target_pairs={{0,2},{2,4},{4,6},{6,0},{1,3},{3,5},{5,7},{7,1},{8,10},{10,12},{12... | collective-permute-start | bytes 43016 | tf_op jit(solution)/shard_map/ppermute | solution.py:28
Sparse Core Ops, SparseCore 0:
  15.2 42.2 reduce-scatter.4
